TPU v7x, 128 devices: a whole 4x4x4 slice. The times are simulated.
128 devices in a mesh: row: 8 (over z, core), col: 16 (over x, y).
Axes of the slice: x: 4, y: 4, z: 4, core: 2. Of those that a mesh axis runs over, the one named last changes fastest.
Arguments:
- points: float32 [64, 32768], P(None, ('row', 'col')), may hold values from -10 to 10
- start: float32 [32768], P(('row', 'col')), may hold values from -6 to 6
Outputs:
- basis: float32 [9, 32768], P(None, ('row', 'col'))
- tridiag: float32 [2, 8], replicated
All inputs are finite; a program needn't handle non-finite values.
Results may differ from a plain program's by a relative error of at most 0.028.
Values may be sent and summed in bfloat16 or wider, within the bound.
No kernel may reach another device: no remote copies, remote signals or barrier semaphores. Data moves between devices by JAX's collectives and lax.ppermute only.
A program may use at most 64 MiB of HBM per device.

v0:
```python
import jax
import jax.numpy as jnp
from jax import lax
from jax.sharding import Mesh
from jax.sharding import PartitionSpec as P

ITERS = 8
COL = ("col_0", "col_1")
ROW = ("row_0", "row_1")
ROW_COL = ("row_0", "row_1", "col_0", "col_1")


def sent_to_all(x, axis):
    count = lax.axis_size(axis)
    return lax.all_to_all(jnp.broadcast_to(x[None], (count, *x.shape)), axis, 0, 0, tiled=True)


def joined_along(pieces, dim):
    pieces = jnp.moveaxis(pieces, 0, dim)
    lengths = pieces.shape
    return pieces.reshape(*lengths[:dim], lengths[dim] * lengths[dim + 1], *lengths[dim + 2 :])


def gather_directly(x, axis, dim):
    pieces = sent_to_all(x, axis)
    return joined_along(pieces, dim)


def cut_along(x, dim, count):
    before, after = (x.shape[:dim], x.shape[dim + 1 :])
    return jnp.moveaxis(x.reshape(*before, count, -1, *after), dim, 0)


def summed_on_arrival(x, axis, dim):
    pieces = cut_along(x, dim, lax.axis_size(axis))
    arrived = lax.all_to_all(pieces, axis, split_axis=0, concat_axis=0, tiled=True)
    return arrived.sum(axis=0)


def taken_together(x, axis):
    return sent_to_all(x, axis).sum(axis=0)


def over_axes(x, axes):
    far, near = axes
    return taken_together(taken_together(x, near), far)


def in_one(arrays, axis):
    ends = [0]
    for a in arrays:
        ends.append(ends[-1] + a.size)
    so_far = over_axes(jnp.concatenate([a.ravel() for a in arrays]), axis)
    return tuple((so_far[b:e].reshape(a.shape) for a, b, e in zip(arrays, ends, ends[1:])))


def kernel_rows(row_pts, col_pts, col_sq, scale):
    cross = lax.dot_general(
        row_pts,
        col_pts,
        (((0,), (0,)), ((), ())),
        precision=lax.Precision.HIGHEST,
        preferred_element_type=jnp.float32,
    )
    row_sq = jnp.sum(row_pts * row_pts, axis=0)
    dist = row_sq[:, None] + col_sq[None, :] - 2.0 * cross
    return jnp.exp(-dist * scale).astype(jnp.bfloat16)


def per_device(points, start):
    feats = points.shape[0]
    count = points.shape[1]
    scale = 0.5 / feats
    col_pts = gather_directly(points, COL, 1)
    row_pts = gather_directly(points, ROW, 1)
    col_sq = jnp.sum(col_pts * col_pts, axis=0)
    width = row_pts.shape[1]
    stored = lax.map(
        lambda pts: kernel_rows(pts, col_pts, col_sq, scale),
        jnp.moveaxis(row_pts.reshape(feats, width // count, count), 1, 0),
    )
    stored = stored.reshape(row_pts.shape[1], col_pts.shape[1])
    start_sq = over_axes(jnp.sum(start * start), ("row_0", ("row_1", "col_0", "col_1")))
    basis = [start / jnp.sqrt(start_sq + 1e-06)]
    alphas = []
    betas = []
    for step in range(ITERS):
        vb = basis[-1].astype(jnp.bfloat16)
        full = gather_directly(vb, COL, 0)
        w = summed_on_arrival(jnp.dot(stored, full, preferred_element_type=jnp.float32), ROW, 0)
        stacked = jnp.stack(basis)
        h1 = over_axes(
            jnp.dot(stacked, w, precision=lax.Precision.HIGHEST),
            ("row_0", ("row_1", "col_0", "col_1")),
        )
        w = w - jnp.dot(h1, stacked, precision=lax.Precision.HIGHEST)
        local = jnp.dot(stacked, w, precision=lax.Precision.HIGHEST)
        h2, before = in_one((local, jnp.sum(w * w)), ("row_0", ("row_1", "col_0", "col_1")))
        w = w - jnp.dot(h2, stacked, precision=lax.Precision.HIGHEST)
        squares = before - jnp.sum(h2 * h2)
        alphas.append(h1[step])
        beta = jnp.sqrt(squares + 1e-06)
        betas.append(beta)
        basis.append(w / beta)
    return (jnp.stack(basis), jnp.stack([jnp.stack(alphas), jnp.stack(betas)]))


def solution(mesh):
    torus = Mesh(mesh.devices.reshape(4, 2, 4, 4), ("row_0", "row_1", "col_0", "col_1"))
    return jax.shard_map(
        per_device,
        mesh=torus,
        in_specs=(P(None, ROW_COL), P(ROW_COL)),
        out_specs=(P(None, ROW_COL), P()),
        check_vma=False,
    )
```

profile of v0, /device:TPU:1, one launch (start us, length us, event | category | flops | bytes accessed | tf_op | source)
XLA Modules:
  0.0 688.6 jit_solution(10382255843997516026)
XLA Ops:
  2.6 15.3 %all_to_all.334 = f32[32,1,1]{2,1,0:T(1,128)S(1)} all-to-all(f32[32,1,1]{2,1,0:T(1,128)S(1)} %broadcast_in_dim.96), channel_id=1, replica_groups=mesh['row_0'=4,'row_1'=2,'col_0'=4,'col_1'=4] {'row_1','col_0','col_1'}, dimensions={0} | all-to-all | bytes 256 | tf_op jit(solution)/shard_map/all_to_all | solution.py:15
  19.1 9.0 %all_to_all.335 = f32[4,1,1]{2,1,0:T(1,128)S(1)} all-to-all(f32[4,1,1]{2,1,0:T(1,128)S(1)} %broadcast_in_dim.97), channel_id=1, replica_groups=mesh['row_0'=4,'row_1'=2,'col_0'=4,'col_1'=4] {'row_0'}, dimensions={0} | all-to-all | bytes 32 | tf_op jit(solution)/shard_map/all_to_all | solution.py:15
  31.2 9.2 %all_to_all.336 = bf16[16,2,128]{2,1,0:T(2,128)(2,1)S(1)} all-to-all(bf16[16,2,128]{2,1,0:T(2,128)(2,1)S(1)} %reshape.510), channel_id=1, replica_groups=mesh['row_0'=4,'row_1'=2,'col_0'=4,'col_1'=4] {'col_0','col_1'}, dimensions={0} | all-to-all | bytes 16384 | tf_op jit(solution)/shard_map/all_to_all | solution.py:15
  41.4 15.9 %all_to_all.337 = f32[16,64,256]{2,1,0:T(8,128)S(1)} all-to-all(f32[16,64,256]{2,1,0:T(8,128)S(1)} %broadcast_in_dim.100), channel_id=1, replica_groups=mesh['row_0'=4,'row_1'=2,'col_0'=4,'col_1'=4] {'col_0','col_1'}, dimensions={0} | all-to-all | bytes 2097152 | tf_op jit(solution)/shard_map/all_to_all | solution.py:15
  58.9 8.3 %all-to-all-start.2 = ((f32[8,64,256]{2,1,0:T(8,128)}), f32[8,64,256]{2,1,0:T(8,128)S(1)}, u32[]{:S(2)}, u32[]{:S(2)}) async-start(f32[8,64,256]{2,1,0:T(8,128)} %broadcast_in_dim.99), calls=%async_computation.2 | async-start | bytes 1048576 | tf_op jit(solution)/shard_map/all_to_all | solution.py:15
  67.4 9.1 %all-to-all-done.2 = f32[8,64,256]{2,1,0:T(8,128)S(1)} async-done(((f32[8,64,256]{2,1,0:T(8,128)}), f32[8,64,256]{2,1,0:T(8,128)S(1)}, u32[]{:S(2)}, u32[]{:S(2)}) %all-to-all-start.2) | async-done | bytes 524320 | tf_op jit(solution)/shard_map/all_to_all | solution.py:15
  76.6 43.6 %while.10 = (s32[]{:T(128)}, bf16[8,256,4096]{2,1,0:T(8,128)(2,1)}, f32[8,64,256]{2,1,0:T(8,128)S(1)}, f32[4096]{0:T(1024)S(1)}, f32[64,4096]{1,0:T(8,128)S(1)}, /*index=5*/s32[]{:T(128)}) while((s32[]{:T(128)}, bf16[8,256,4096]{2,1,0:T(8,128)(2,1)}, f32[8,64,256]{2,1,0:T(8,128)S(1)}, f32[4096]{0:T(1024)S(1)}, f32[64,4096]{1,0:T(8,128)S(1)}, ...), condition=%wide.region_6.7_spmd, body=%wide.region_4.6_spmd.sunk | while | flops 811630336 | bytes 3296329 | solution.py:78
  120.1 10.2 %fusion.56 = f32[1,8,256]{2,0,1:T(1,128)S(1)} fusion(bf16[8,256,4096]{2,1,0:T(8,128)(2,1)} %get-tuple-element.29, bf16[4096,1,1]{0,1,2:T(2,128)(2,1)S(1)} %bitcast.270), kind=kOutput, calls=%fused_computation.121 | convolution fusion | flops 16777216 | bytes 16793600 | tf_op jit(solution)/shard_map/dot_general | solution.py:90
  130.4 7.9 %all_to_all.338 = f32[8,1,256]{2,1,0:T(1,128)S(1)} all-to-all(f32[8,1,256]{2,1,0:T(1,128)S(1)} %all_to_all.227), channel_id=1, replica_groups=mesh['row_0'=4,'row_1'=2,'col_0'=4,'col_1'=4] {'row_0','row_1'}, dimensions={0} | all-to-all | bytes 16384 | tf_op jit(solution)/shard_map/all_to_all | solution.py:36
  139.6 10.9 %all_to_all.339 = f32[32,1,1]{2,1,0:T(1,128)S(1)} all-to-all(f32[32,1,1]{2,1,0:T(1,128)S(1)} %broadcast_in_dim.102), channel_id=1, replica_groups=mesh['row_0'=4,'row_1'=2,'col_0'=4,'col_1'=4] {'row_1','col_0','col_1'}, dimensions={0} | all-to-all | bytes 256 | tf_op jit(solution)/shard_map/all_to_all | solution.py:15
  151.8 6.5 all_to_all.340
  161.4 11.8 %all_to_all.341 = f32[32,1,2]{2,1,0:T(1,128)S(1)} all-to-all(f32[32,1,2]{2,1,0:T(1,128)S(1)} %broadcast_in_dim.104), channel_id=1, replica_groups=mesh['row_0'=4,'row_1'=2,'col_0'=4,'col_1'=4] {'row_1','col_0','col_1'}, dimensions={0} | all-to-all | bytes 512 | tf_op jit(solution)/shard_map/all_to_all | solution.py:15
  173.3 6.5 all_to_all.342
  184.2 9.6 %all_to_all.343 = bf16[16,2,128]{2,1,0:T(2,128)(2,1)S(1)} all-to-all(bf16[16,2,128]{2,1,0:T(2,128)(2,1)S(1)} %reshape.512), channel_id=1, replica_groups=mesh['row_0'=4,'row_1'=2,'col_0'=4,'col_1'=4] {'col_0','col_1'}, dimensions={0} | all-to-all | bytes 16384 | tf_op jit(solution)/shard_map/all_to_all | solution.py:15
  193.8 10.2 %fusion.57 = f32[1,8,256]{2,0,1:T(1,128)S(1)} fusion(bf16[8,256,4096]{2,1,0:T(8,128)(2,1)} %get-tuple-element.29, bf16[4096,1,1]{0,1,2:T(2,128)(2,1)S(1)} %bitcast.273), kind=kOutput, calls=%fused_computation.122 | convolution fusion | flops 16777216 | bytes 16793600 | tf_op jit(solution)/shard_map/dot_general | solution.py:90
  204.1 10.2 %all_to_all.344 = f32[8,1,256]{2,1,0:T(1,128)S(1)} all-to-all(f32[8,1,256]{2,1,0:T(1,128)S(1)} %all_to_all.234), channel_id=1, replica_groups=mesh['row_0'=4,'row_1'=2,'col_0'=4,'col_1'=4] {'row_0','row_1'}, dimensions={0} | all-to-all | bytes 16384 | tf_op jit(solution)/shard_map/all_to_all | solution.py:36
  214.5 10.7 %all_to_all.345 = f32[32,1,2]{2,1,0:T(1,128)S(1)} all-to-all(f32[32,1,2]{2,1,0:T(1,128)S(1)} %broadcast_in_dim.107), channel_id=1, replica_groups=mesh['row_0'=4,'row_1'=2,'col_0'=4,'col_1'=4] {'row_1','col_0','col_1'}, dimensions={0} | all-to-all | bytes 512 | tf_op jit(solution)/shard_map/all_to_all | solution.py:15
  225.2 6.5 all_to_all.346
  233.3 11.8 %all_to_all.347 = f32[32,1,3]{2,1,0:T(1,128)S(1)} all-to-all(f32[32,1,3]{2,1,0:T(1,128)S(1)} %broadcast_in_dim.109), channel_id=1, replica_groups=mesh['row_0'=4,'row_1'=2,'col_0'=4,'col_1'=4] {'row_1','col_0','col_1'}, dimensions={0} | all-to-all | bytes 768 | tf_op jit(solution)/shard_map/all_to_all | solution.py:15
  255.1 9.2 %all_to_all.349 = bf16[16,2,128]{2,1,0:T(2,128)(2,1)S(1)} all-to-all(bf16[16,2,128]{2,1,0:T(2,128)(2,1)S(1)} %reshape.514), channel_id=1, replica_groups=mesh['row_0'=4,'row_1'=2,'col_0'=4,'col_1'=4] {'col_0','col_1'}, dimensions={0} | all-to-all | bytes 16384 | tf_op jit(solution)/shard_map/all_to_all | solution.py:15
  264.3 10.2 %fusion.58 = f32[1,8,256]{2,0,1:T(1,128)S(1)} fusion(bf16[8,256,4096]{2,1,0:T(8,128)(2,1)} %get-tuple-element.29, bf16[4096,1,1]{0,1,2:T(2,128)(2,1)S(1)} %bitcast.274), kind=kOutput, calls=%fused_computation.123 | convolution fusion | flops 16777216 | bytes 16793600 | tf_op jit(solution)/shard_map/dot_general | solution.py:90
  274.5 10.2 %all_to_all.350 = f32[8,1,256]{2,1,0:T(1,128)S(1)} all-to-all(f32[8,1,256]{2,1,0:T(1,128)S(1)} %all_to_all.241), channel_id=1, replica_groups=mesh['row_0'=4,'row_1'=2,'col_0'=4,'col_1'=4] {'row_0','row_1'}, dimensions={0} | all-to-all | bytes 16384 | tf_op jit(solution)/shard_map/all_to_all | solution.py:36
  284.9 10.6 %all_to_all.351 = f32[32,1,3]{2,1,0:T(1,128)S(1)} all-to-all(f32[32,1,3]{2,1,0:T(1,128)S(1)} %broadcast_in_dim.112), channel_id=1, replica_groups=mesh['row_0'=4,'row_1'=2,'col_0'=4,'col_1'=4] {'row_1','col_0','col_1'}, dimensions={0} | all-to-all | bytes 768 | tf_op jit(solution)/shard_map/all_to_all | solution.py:15
  303.7 11.8 %all_to_all.353 = f32[32,1,4]{2,1,0:T(1,128)S(1)} all-to-all(f32[32,1,4]{2,1,0:T(1,128)S(1)} %broadcast_in_dim.114), channel_id=1, replica_groups=mesh['row_0'=4,'row_1'=2,'col_0'=4,'col_1'=4] {'row_1','col_0','col_1'}, dimensions={0} | all-to-all | bytes 1024 | tf_op jit(solution)/shard_map/all_to_all | solution.py:15
  325.4 9.3 %all_to_all.355 = bf16[16,2,128]{2,1,0:T(2,128)(2,1)S(1)} all-to-all(bf16[16,2,128]{2,1,0:T(2,128)(2,1)S(1)} %reshape.516), channel_id=1, replica_groups=mesh['row_0'=4,'row_1'=2,'col_0'=4,'col_1'=4] {'col_0','col_1'}, dimensions={0} | all-to-all | bytes 16384 | tf_op jit(solution)/shard_map/all_to_all | solution.py:15
  334.7 10.2 %fusion.59 = f32[1,8,256]{2,0,1:T(1,128)S(1)} fusion(bf16[8,256,4096]{2,1,0:T(8,128)(2,1)} %get-tuple-element.29, bf16[4096,1,1]{0,1,2:T(2,128)(2,1)S(1)} %bitcast.275), kind=kOutput, calls=%fused_computation.124 | convolution fusion | flops 16777216 | bytes 16793600 | tf_op jit(solution)/shard_map/dot_general | solution.py:90
  344.9 10.2 %all_to_all.356 = f32[8,1,256]{2,1,0:T(1,128)S(1)} all-to-all(f32[8,1,256]{2,1,0:T(1,128)S(1)} %all_to_all.248), channel_id=1, replica_groups=mesh['row_0'=4,'row_1'=2,'col_0'=4,'col_1'=4] {'row_0','row_1'}, dimensions={0} | all-to-all | bytes 16384 | tf_op jit(solution)/shard_map/all_to_all | solution.py:36
  355.4 10.7 %all_to_all.357 = f32[32,1,4]{2,1,0:T(1,128)S(1)} all-to-all(f32[32,1,4]{2,1,0:T(1,128)S(1)} %broadcast_in_dim.117), channel_id=1, replica_groups=mesh['row_0'=4,'row_1'=2,'col_0'=4,'col_1'=4] {'row_1','col_0','col_1'}, dimensions={0} | all-to-all | bytes 1024 | tf_op jit(solution)/shard_map/all_to_all | solution.py:15
  374.2 11.8 %all_to_all.359 = f32[32,1,5]{2,1,0:T(1,128)S(1)} all-to-all(f32[32,1,5]{2,1,0:T(1,128)S(1)} %broadcast_in_dim.119), channel_id=1, replica_groups=mesh['row_0'=4,'row_1'=2,'col_0'=4,'col_1'=4] {'row_1','col_0','col_1'}, dimensions={0} | all-to-all | bytes 1280 | tf_op jit(solution)/shard_map/all_to_all | solution.py:15
  395.9 9.2 %all_to_all.361 = bf16[16,2,128]{2,1,0:T(2,128)(2,1)S(1)} all-to-all(bf16[16,2,128]{2,1,0:T(2,128)(2,1)S(1)} %reshape.518), channel_id=1, replica_groups=mesh['row_0'=4,'row_1'=2,'col_0'=4,'col_1'=4] {'col_0','col_1'}, dimensions={0} | all-to-all | bytes 16384 | tf_op jit(solution)/shard_map/all_to_all | solution.py:15
  405.1 10.2 %fusion.60 = f32[1,8,256]{2,0,1:T(1,128)S(1)} fusion(bf16[8,256,4096]{2,1,0:T(8,128)(2,1)} %get-tuple-element.29, bf16[4096,1,1]{0,1,2:T(2,128)(2,1)S(1)} %bitcast.276), kind=kOutput, calls=%fused_computation.125 | convolution fusion | flops 16777216 | bytes 16793600 | tf_op jit(solution)/shard_map/dot_general | solution.py:90
  415.9 6.5 all-to-all-start.29
  427.2 10.6 %all_to_all.362 = f32[32,1,5]{2,1,0:T(1,128)S(1)} all-to-all(f32[32,1,5]{2,1,0:T(1,128)S(1)} %broadcast_in_dim.122), channel_id=1, replica_groups=mesh['row_0'=4,'row_1'=2,'col_0'=4,'col_1'=4] {'row_1','col_0','col_1'}, dimensions={0} | all-to-all | bytes 1280 | tf_op jit(solution)/shard_map/all_to_all | solution.py:15
  446.0 11.8 %all_to_all.364 = f32[32,1,6]{2,1,0:T(1,128)S(1)} all-to-all(f32[32,1,6]{2,1,0:T(1,128)S(1)} %broadcast_in_dim.124), channel_id=1, replica_groups=mesh['row_0'=4,'row_1'=2,'col_0'=4,'col_1'=4] {'row_1','col_0','col_1'}, dimensions={0} | all-to-all | bytes 1536 | tf_op jit(solution)/shard_map/all_to_all | solution.py:15
  467.6 9.4 %all_to_all.366 = bf16[16,2,128]{2,1,0:T(2,128)(2,1)S(1)} all-to-all(bf16[16,2,128]{2,1,0:T(2,128)(2,1)S(1)} %reshape.520), channel_id=1, replica_groups=mesh['row_0'=4,'row_1'=2,'col_0'=4,'col_1'=4] {'col_0','col_1'}, dimensions={0} | all-to-all | bytes 16384 | tf_op jit(solution)/shard_map/all_to_all | solution.py:15
  477.0 10.2 %fusion.61 = f32[1,8,256]{2,0,1:T(1,128)S(1)} fusion(bf16[8,256,4096]{2,1,0:T(8,128)(2,1)} %get-tuple-element.29, bf16[4096,1,1]{0,1,2:T(2,128)(2,1)S(1)} %bitcast.277), kind=kOutput, calls=%fused_computation.126 | convolution fusion | flops 16777216 | bytes 16793600 | tf_op jit(solution)/shard_map/dot_general | solution.py:90
  487.8 6.5 all-to-all-start.35
  499.1 10.7 %all_to_all.367 = f32[32,1,6]{2,1,0:T(1,128)S(1)} all-to-all(f32[32,1,6]{2,1,0:T(1,128)S(1)} %broadcast_in_dim.127), channel_id=1, replica_groups=mesh['row_0'=4,'row_1'=2,'col_0'=4,'col_1'=4] {'row_1','col_0','col_1'}, dimensions={0} | all-to-all | bytes 1536 | tf_op jit(solution)/shard_map/all_to_all | solution.py:15
  518.0 11.8 %all_to_all.369 = f32[32,1,7]{2,1,0:T(1,128)S(1)} all-to-all(f32[32,1,7]{2,1,0:T(1,128)S(1)} %broadcast_in_dim.129), channel_id=1, replica_groups=mesh['row_0'=4,'row_1'=2,'col_0'=4,'col_1'=4] {'row_1','col_0','col_1'}, dimensions={0} | all-to-all | bytes 1792 | tf_op jit(solution)/shard_map/all_to_all | solution.py:15
  539.6 9.2 %all_to_all.371 = bf16[16,2,128]{2,1,0:T(2,128)(2,1)S(1)} all-to-all(bf16[16,2,128]{2,1,0:T(2,128)(2,1)S(1)} %reshape.522), channel_id=1, replica_groups=mesh['row_0'=4,'row_1'=2,'col_0'=4,'col_1'=4] {'col_0','col_1'}, dimensions={0} | all-to-all | bytes 16384 | tf_op jit(solution)/shard_map/all_to_all | solution.py:15
  548.8 10.2 %fusion.62 = f32[1,8,256]{2,0,1:T(1,128)S(1)} fusion(bf16[8,256,4096]{2,1,0:T(8,128)(2,1)} %get-tuple-element.29, bf16[4096,1,1]{0,1,2:T(2,128)(2,1)S(1)} %bitcast.278), kind=kOutput, calls=%fused_computation.127 | convolution fusion | flops 16777216 | bytes 16793600 | tf_op jit(solution)/shard_map/dot_general | solution.py:90
  559.6 6.5 all-to-all-start.41
  570.9 10.6 %all_to_all.372 = f32[32,1,7]{2,1,0:T(1,128)S(1)} all-to-all(f32[32,1,7]{2,1,0:T(1,128)S(1)} %broadcast_in_dim.132), channel_id=1, replica_groups=mesh['row_0'=4,'row_1'=2,'col_0'=4,'col_1'=4] {'row_1','col_0','col_1'}, dimensions={0} | all-to-all | bytes 1792 | tf_op jit(solution)/shard_map/all_to_all | solution.py:15
  589.7 11.8 %all_to_all.374 = f32[32,1,8]{2,1,0:T(1,128)S(1)} all-to-all(f32[32,1,8]{2,1,0:T(1,128)S(1)} %broadcast_in_dim.134), channel_id=1, replica_groups=mesh['row_0'=4,'row_1'=2,'col_0'=4,'col_1'=4] {'row_1','col_0','col_1'}, dimensions={0} | all-to-all | bytes 2048 | tf_op jit(solution)/shard_map/all_to_all | solution.py:15
  611.5 9.4 %all_to_all.376 = bf16[16,2,128]{2,1,0:T(2,128)(2,1)S(1)} all-to-all(bf16[16,2,128]{2,1,0:T(2,128)(2,1)S(1)} %reshape.524), channel_id=1, replica_groups=mesh['row_0'=4,'row_1'=2,'col_0'=4,'col_1'=4] {'col_0','col_1'}, dimensions={0} | all-to-all | bytes 16384 | tf_op jit(solution)/shard_map/all_to_all | solution.py:15
  620.9 10.2 %fusion.63 = f32[1,8,256]{2,0,1:T(1,128)S(1)} fusion(bf16[8,256,4096]{2,1,0:T(8,128)(2,1)} %get-tuple-element.29, bf16[4096,1,1]{0,1,2:T(2,128)(2,1)S(1)} %bitcast.271), kind=kOutput, calls=%fused_computation.128 | convolution fusion | flops 16777216 | bytes 16793600 | tf_op jit(solution)/shard_map/dot_general | solution.py:90
  631.7 6.5 all-to-all-start.47
  643.0 10.7 %all_to_all.377 = f32[32,1,8]{2,1,0:T(1,128)S(1)} all-to-all(f32[32,1,8]{2,1,0:T(1,128)S(1)} %broadcast_in_dim.137), channel_id=1, replica_groups=mesh['row_0'=4,'row_1'=2,'col_0'=4,'col_1'=4] {'row_1','col_0','col_1'}, dimensions={0} | all-to-all | bytes 2048 | tf_op jit(solution)/shard_map/all_to_all | solution.py:15
  (252 shorter events, 209.6 us)
Async XLA Ops:
  58.9 17.7 %all-to-all-start.2 = ((f32[8,64,256]{2,1,0:T(8,128)}), f32[8,64,256]{2,1,0:T(8,128)S(1)}, u32[]{:S(2)}, u32[]{:S(2)}) async-start(f32[8,64,256]{2,1,0:T(8,128)} %broadcast_in_dim.99), calls=%async_computation.2 | async-start | bytes 1048576 | tf_op jit(solution)/shard_map/all_to_all | solution.py:15
  415.9 11.1 %all-to-all-start.29 = ((f32[8,1,256]{2,1,0:T(1,128)}), f32[8,1,256]{2,1,0:T(1,128)S(1)}, u32[]{:S(2)}, u32[]{:S(2)}) async-start(f32[8,1,256]{2,1,0:T(1,128)} %all_to_all.255), calls=%async_computation.29 | async-start | bytes 16384 | tf_op jit(solution)/shard_map/all_to_all | solution.py:36
  487.8 11.1 %all-to-all-start.35 = ((f32[8,1,256]{2,1,0:T(1,128)}), f32[8,1,256]{2,1,0:T(1,128)S(1)}, u32[]{:S(2)}, u32[]{:S(2)}) async-start(f32[8,1,256]{2,1,0:T(1,128)} %all_to_all.262), calls=%async_computation.35 | async-start | bytes 16384 | tf_op jit(solution)/shard_map/all_to_all | solution.py:36
  559.6 11.1 %all-to-all-start.41 = ((f32[8,1,256]{2,1,0:T(1,128)}), f32[8,1,256]{2,1,0:T(1,128)S(1)}, u32[]{:S(2)}, u32[]{:S(2)}) async-start(f32[8,1,256]{2,1,0:T(1,128)} %all_to_all.269), calls=%async_computation.41 | async-start | bytes 16384 | tf_op jit(solution)/shard_map/all_to_all | solution.py:36
  631.7 11.1 %all-to-all-start.47 = ((f32[8,1,256]{2,1,0:T(1,128)}), f32[8,1,256]{2,1,0:T(1,128)S(1)}, u32[]{:S(2)}, u32[]{:S(2)}) async-start(f32[8,1,256]{2,1,0:T(1,128)} %all_to_all.276), calls=%async_computation.47 | async-start | bytes 16384 | tf_op jit(solution)/shard_map/all_to_all | solution.py:36
  662.5 12.2 %all-to-all-start.50 = ((f32[32,1,9]{2,1,0:T(1,128)}), f32[32,1,9]{2,1,0:T(1,128)S(1)}, u32[]{:S(2)}, u32[]{:S(2)}) async-start(f32[32,1,9]{2,1,0:T(1,128)} %broadcast_in_dim.139), calls=%async_computation.50 | async-start | bytes 32768 | tf_op jit(solution)/shard_map/all_to_all | solution.py:15
  675.3 8.3 %all-to-all-start.51 = ((f32[4,1,9]{2,1,0:T(1,128)}), f32[4,1,9]{2,1,0:T(1,128)S(1)}, u32[]{:S(2)}, u32[]{:S(2)}) async-start(f32[4,1,9]{2,1,0:T(1,128)} %broadcast_in_dim.140), calls=%async_computation.51 | async-start | bytes 4096 | tf_op jit(solution)/shard_map/all_to_all | solution.py:15
where the time goes:
time: 698 us; the launch traced here: 689 us
  blocking collectives  418 us (60%)
  matrix products  128 us (18%)
  starting transfers between devices  42.9 us (6%)
  waiting for transfers between devices  30.1 us (4%)
  other arithmetic  29.9 us (4%)
  local copies, waits for them, and re-layouts  25.6 us (4%)
  between operations  13.5 us (2%)
    all_to_all x41, blocking collectives, sent_to_all(): lax.all_to_all(jnp.broadcast_to(x[None], (count, *x.shape)), axis, 0, 0,...  380 us
    dot_general x8, matrix products, per_device(): jnp.dot(stored, full, preferred_element_type=jnp.float32)  81.5 us
    dot_general x8, matrix products, kernel_rows(): lax.dot_general(row_pts, col_pts, (((0,), (0,)), ((), ())), precision=lax...  43.3 us
    all_to_all x4, blocking collectives, summed_on_arrival(): lax.all_to_all(pieces, axis, split_axis=0, concat_axis=0, tiled=True)  38.6 us
    all_to_all x4, starting transfers between devices, summed_on_arrival(): lax.all_to_all(pieces, axis, split_axis=0, concat_axis=0, tiled=True)  25.9 us
    all_to_all x4, waiting for transfers between devices, summed_on_arrival(): lax.all_to_all(pieces, axis, split_axis=0, concat_axis=0, tiled=True)  18.5 us
    all_to_all x3, starting transfers between devices, sent_to_all(): lax.all_to_all(jnp.broadcast_to(x[None], (count, *x.shape)), axis, 0, 0,...  17 us
  transfers between devices with their start and end apart: 7, of which 6 were waited for; matrix products, arithmetic and copies ran while one was open for 1% of the time, Pallas kernels for 0%

commit v1 on v0

v1 whole, which is shorter than its diff:
```python
import jax
import jax.numpy as jnp
from jax import lax
from jax.experimental import pallas as pl
from jax.experimental.pallas import tpu as pltpu
from jax.sharding import Mesh
from jax.sharding import PartitionSpec as P

ITERS = 8
FEATS = 64
LANES = 128
OWN = 256
CHIPS = 64
DEVICES = 128
CODE = 12.0
ALL = ("z", "core", "x", "y")
CHIP = ("z", "x", "y")
LOG2E = 1.4426950408889634
ROWS = DEVICES * OWN // LANES
VEC_ROWS = 16
BLOCK = LANES + VEC_ROWS
VMEM = pl.BlockSpec(memory_space=pltpu.VMEM)


def parts_of(x):
    hi = x.astype(jnp.bfloat16)
    rest = x - hi.astype(jnp.float32)
    mid = rest.astype(jnp.bfloat16)
    low = (rest - mid.astype(jnp.float32)).astype(jnp.bfloat16)
    return hi, mid, low


def prepare(points_ref, start_ref, sent_ref, wa_ref, wb_ref):
    x = points_ref[...]
    code = jnp.exp2(x * CODE).T
    sent_ref[:LANES, :] = jnp.concatenate([code[:LANES], code[LANES:]], axis=1).astype(jnp.bfloat16)
    s0, s1, s2 = parts_of(start_ref[...])
    pad = jnp.zeros((VEC_ROWS - 6, LANES), jnp.bfloat16)
    sent_ref[LANES:, :] = jnp.concatenate([s0, s1, s2, pad], axis=0)
    scale = LOG2E / FEATS
    w = x * scale
    whi = w.astype(jnp.bfloat16)
    wlo = (w - whi.astype(jnp.float32)).astype(jnp.bfloat16)
    half = jnp.sum(x * x, axis=0, keepdims=True) * (-0.5 * scale)
    h0, h1, h2 = (jnp.broadcast_to(h.astype(jnp.float32), (FEATS, OWN)) for h in parts_of(half))
    row = lax.broadcasted_iota(jnp.int32, (FEATS, OWN), 0)
    zero = jnp.zeros((FEATS, OWN), jnp.float32)
    own = jnp.where(row == 0, h0, jnp.where(row == 1, h1, jnp.where(row == 2, h2, zero))).astype(jnp.bfloat16)
    wa_ref[...] = jnp.concatenate([whi, whi, wlo, own], axis=0)
    wb_ref[...] = jnp.concatenate([whi, whi, own, wlo], axis=0)


def build(points_ref, wa_ref, wb_ref, out_ref):
    scale = LOG2E / FEATS
    low_half = lax.broadcasted_iota(jnp.int32, (LANES, LANES), 1) < FEATS
    ones = jnp.ones((LANES, LANES), jnp.float32)

    def chip(p, carry):
        code = points_ref[p, :LANES, :].astype(jnp.float32)
        x = jnp.log2(code) * (1.0 / CODE)
        hi = x.astype(jnp.bfloat16).astype(jnp.float32)
        lo = x - hi
        swapped = pltpu.roll(lo, FEATS, 1)
        xx = x * x * (0.5 * scale)
        sq_a = jnp.sum(jnp.where(low_half, xx, 0.0), axis=1, keepdims=True)
        sq_b = jnp.sum(jnp.where(low_half, 0.0, xx), axis=1, keepdims=True)
        a = jnp.concatenate([jnp.where(low_half, hi, swapped), jnp.where(low_half, hi, ones)], axis=1)
        b = jnp.concatenate([jnp.where(low_half, swapped, hi), jnp.where(low_half, ones, hi)], axis=1)
        at = pl.ds(pl.multiple_of((p // 4) * LANES, LANES), LANES)
        s = 2 * (p % 4)
        ea = jnp.dot(a.astype(jnp.bfloat16), wa_ref[...], preferred_element_type=jnp.float32)
        out_ref[s, at, :] = jnp.exp2(ea - sq_a).astype(jnp.bfloat16)
        eb = jnp.dot(b.astype(jnp.bfloat16), wb_ref[...], preferred_element_type=jnp.float32)
        out_ref[s + 1, at, :] = jnp.exp2(eb - sq_b).astype(jnp.bfloat16)
        return carry

    lax.fori_loop(0, CHIPS, chip, 0, unroll=2)


def total(x):
    return jnp.sum(jnp.sum(x.reshape(-1, 8, LANES), axis=0), keepdims=True)


def product(q_ref, mine_ref, other_ref, out_ref):
    core = lax.axis_index("core")
    row = lax.broadcasted_iota(jnp.int32, (8, OWN), 0)
    acc = jnp.zeros((8, OWN), jnp.float32)
    for held, which in ((mine_ref, core), (other_ref, 1 - core)):
        cols = []
        for z in range(4):
            for k in range(4):
                at = pl.multiple_of(z * 64 + which * 32 + 8 * k, 8)
                cols.append(q_ref[pl.ds(at, 8), :])
        q = jnp.concatenate(cols, axis=1).astype(jnp.bfloat16)
        for s in range(8):
            got = jnp.dot(q, held[s], preferred_element_type=jnp.float32)
            acc = acc + jnp.where(row == s, got, 0.0)
    w = jnp.sum(acc, axis=0, keepdims=True)
    w = jnp.concatenate([w[:, :LANES], w[:, LANES:]], axis=0)
    out_ref[...] = jnp.broadcast_to(w[None], out_ref.shape)


def first_step(mine_vec_ref, other_vec_ref, mine_ref, other_ref, q_ref, kept_ref, w_ref):
    kept_ref[...] = jnp.zeros((2, LANES), jnp.float32)
    core = lax.axis_index("core")
    for held, which in ((mine_vec_ref, core), (other_vec_ref, 1 - core)):
        for p in range(CHIPS):
            v = held[p].astype(jnp.float32)
            at = (p // 16) * 64 + which * 32 + (p % 16) * 2
            q_ref[pl.ds(at, 2), :] = v[0:2] + v[2:4] + v[4:6]
    start = q_ref[...]
    q_ref[...] = start / jnp.sqrt(total(start * start) + 1e-6)
    product(q_ref, mine_ref, other_ref, w_ref)


def orthogonalized(w, basis):
    h1 = [total(q[...] * w) for q in basis]
    for h, q in zip(h1, basis):
        w = w - h * q[...]
    h2 = [total(q[...] * w) for q in basis]
    for h, q in zip(h2, basis):
        w = w - h * q[...]
    beta = jnp.sqrt(total(w * w) + 1e-6)
    return w / beta, h1[-1], beta


def note(found_ref, kept_ref, step, alpha, beta):
    width = kept_ref.shape[1]
    lane = lax.broadcasted_iota(jnp.int32, (1, width), 1)
    kept_ref[0:1, :] = jnp.where(lane == step, alpha, found_ref[0:1, :width])
    kept_ref[1:2, :] = jnp.where(lane == step, beta, found_ref[1:2, :width])


def later_step(*refs):
    count = len(refs) - 7
    w_ref, found_ref, basis, mine_ref, other_ref = refs[0], refs[1], refs[2 : 2 + count], refs[2 + count], refs[3 + count]
    q_ref, kept_ref, out_ref = refs[4 + count :]
    q, alpha, beta = orthogonalized(w_ref[...], basis)
    q_ref[...] = q
    note(found_ref, kept_ref, count - 1, alpha, beta)
    product(q_ref, mine_ref, other_ref, out_ref)


def last_step(*refs):
    w_ref, found_ref, basis, own_ref, kept_ref = refs[0], refs[1], refs[2:-2], refs[-2], refs[-1]
    q, alpha, beta = orthogonalized(w_ref[...], basis)
    note(found_ref, kept_ref, len(basis) - 1, alpha, beta)
    z, core, x, y = (lax.axis_index(a) for a in ALL)
    device = ((z * 2 + core) * 4 + x) * 4 + y
    mask = lax.broadcasted_iota(jnp.int32, (ROWS, LANES), 0)
    for i, held in enumerate(basis):
        for h in range(2):
            own_ref[i : i + 1, h * LANES : (h + 1) * LANES] = held[pl.ds(2 * device + h, 1), :]
    for h in range(2):
        row = jnp.where(mask == 2 * device + h, q, 0.0)
        own_ref[len(basis) :, h * LANES : (h + 1) * LANES] = jnp.sum(row, axis=0, keepdims=True)


def exchanged(x, axis):
    return lax.all_to_all(x, axis, 0, 0, tiled=True)


def sent_to_all(x, axis):
    return exchanged(jnp.broadcast_to(x[None], (lax.axis_size(axis), *x.shape)), axis)


def kept(shape, dtype):
    return pltpu.VMEM(shape, dtype)


def call(body, outs, *args, limit=24 * 2**20):
    return pl.pallas_call(
        body,
        out_shape=outs,
        in_specs=[VMEM] * len(args),
        out_specs=[VMEM] * len(outs),
        compiler_params=pltpu.CompilerParams(vmem_limit_bytes=limit),
    )(*args)


def per_device(points, start):
    f32, bf16 = jnp.float32, jnp.bfloat16
    sent, wa, wb = call(
        prepare,
        (
            jax.ShapeDtypeStruct((BLOCK, LANES), bf16),
            jax.ShapeDtypeStruct((OWN, OWN), bf16),
            jax.ShapeDtypeStruct((OWN, OWN), bf16),
        ),
        points,
        start.reshape(2, LANES),
    )
    mine = sent_to_all(sent, CHIP)
    other = lax.ppermute(mine, "core", [(0, 1), (1, 0)])
    slab = kept((8, CHIPS * OWN // 8, OWN), bf16)
    (mine_k,) = call(build, (slab,), mine, wa, wb)
    (other_k,) = call(build, (slab,), other, wa, wb)
    vector = jax.ShapeDtypeStruct((ROWS, LANES), f32)
    pair = jax.ShapeDtypeStruct((2, LANES), f32)
    spread = jax.ShapeDtypeStruct((DEVICES, 2, LANES), f32)
    q, heads, w = call(first_step, (vector, pair, spread), mine[:, LANES:], other[:, LANES:], mine_k, other_k)
    basis = [q]
    for _ in range(ITERS - 1):
        full = exchanged(w, ALL).reshape(ROWS, LANES)
        q, heads, w = call(later_step, (vector, pair, spread), full, heads, *basis, mine_k, other_k)
        basis.append(q)
    full = exchanged(w, ALL).reshape(ROWS, LANES)
    own, heads = call(last_step, (jax.ShapeDtypeStruct((ITERS + 1, OWN), f32), jax.ShapeDtypeStruct((2, ITERS), f32)), full, heads, *basis)
    return own, heads


def solution(mesh):
    torus = Mesh(mesh.devices.reshape(4, 2, 4, 4), ALL)
    return jax.shard_map(
        per_device,
        mesh=torus,
        in_specs=(P(None, ALL), P(ALL)),
        out_specs=(P(None, ALL), P()),
        check_vma=False,
    )
```

time: 698 us -> 206 us (0.30); the launches traced: 689 us -> 205 us
  blocking collectives: 418 us -> 157 us
  matrix products: 128 us -> 0 us
  Pallas kernels: 0 us -> 43.5 us
  starting transfers between devices: 42.9 us -> 2.19 us
  waiting for transfers between devices: 30.1 us -> 0.01 us
  other arithmetic: 29.9 us -> 0 us
  local copies, waits for them, and re-layouts: 25.6 us -> 1.85 us
  between operations: 13.5 us -> 0.75 us
    all_to_all x45 -> x9, blocking collectives: 418 us -> 157 us  [exchanged(): return lax.all_to_all(x, axis, 0, 0, tiled=True)]
    dot_general x44 -> x0, matrix products: 128 us -> none  [the longest x8 81.5 us: per_device(): jnp.dot(stored, full, preferred_element_type=jnp.float32)]
    pallas_call x0 -> x12, Pallas kernels: none -> 43.5 us  [call(): pl.pallas_call(body, out_shape=outs, in_specs=[VMEM] * len(args), out_spe...]
    all_to_all x7 -> x0, starting transfers between devices: 42.9 us -> none  [the longest x4 25.9 us: summed_on_arrival(): lax.all_to_all(pieces, axis, split_axis=0, concat_axis=0, tiled=True)]
    all_to_all x7 -> x0, waiting for transfers between devices: 30.1 us -> none  [the longest x4 18.5 us: summed_on_arrival(): lax.all_to_all(pieces, axis, split_axis=0, concat_axis=0, tiled=True)]
    reduce_sum x66 -> x0, other arithmetic: 14.1 us -> none  [the longest x7 4.45 us: per_device(): squares = before - jnp.sum(h2 * h2)]
    slice x15 -> x2, local copies, waits for them, and re-layouts: 8.97 us -> 0.04 us  [the longest x1 0.02 us: per_device(): other[:, LANES:]]
  transfers between devices with their start and end apart: 7 -> 1, of which waited for: 6 -> 0; matrix products, arithmetic and copies ran while one was open for 1% -> 0% of each run, Pallas kernels for 0% -> 5%
where the time goes in v1:
time: 206 us; the launch traced here: 205 us
  blocking collectives  157 us (76%)
  Pallas kernels  43.5 us (21%)
  starting transfers between devices  2.19 us (1%)
    all_to_all x9, blocking collectives, exchanged(): return lax.all_to_all(x, axis, 0, 0, tiled=True)  157 us
    pallas_call x12, Pallas kernels, call(): pl.pallas_call(body, out_shape=outs, in_specs=[VMEM] * len(args), out_spe...  43.5 us
  transfers between devices with their start and end apart: 1, of which 0 were waited for; matrix products, arithmetic and copies ran while one was open for 0% of the time, Pallas kernels for 5%

profile of v1, /device:TPU:1, one launch (start us, length us, event | category | flops | bytes accessed | tf_op | source)
XLA Modules:
  0.0 205.2 jit_solution(14121791271356751133)
XLA Ops:
  0.6 0.0 copy-start
  0.6 0.8 copy-done
  1.5 0.0 copy-start.1
  1.5 0.7 copy-done.1
  2.1 0.2 shard_map.41
  2.3 0.3 broadcast_in_dim.2
  2.6 43.5 %all_to_all.45.points_ref = bf16[64,144,128]{2,1,0:T(8,128)(2,1)S(1)} all-to-all(bf16[64,144,128]{2,1,0:T(8,128)(2,1)S(1)} %broadcast_in_dim.2), channel_id=1, replica_groups=mesh['z'=4,'core'=2,'x'=4,'y'=4] {'z','x','y'}, dimensions={0} | all-to-all | bytes 4718592 | tf_op jit(solution)/shard_map/all_to_all | solution.py:160
  46.2 2.2 %collective-permute-start = (bf16[64,144,128]{2,1,0:T(8,128)(2,1)S(1)}, bf16[64,144,128]{2,1,0:T(8,128)(2,1)S(1)}, u32[]{:S(2)}, u32[]{:S(2)}) collective-permute-start(bf16[64,144,128]{2,1,0:T(8,128)(2,1)S(1)} %all_to_all.45.points_ref), channel_id=1, source_target_pairs={{0,16},{16,0},{1,17},{17,1},{2,18},{18,2},{3,19},{19,3},{4,20},{20... | collective-permute-start | bytes 7077896 | tf_op jit(solution)/shard_map/ppermute | solution.py:194
  48.4 9.7 %shard_map.42.mine_ref.refs_3_.refs_4_.refs_5_.refs_6_.refs_7_.refs_8_.refs_9_ = bf16[8,2048,256]{2,1,0:T(8,128)(2,1)S(1)} custom-call(bf16[64,144,128]{2,1,0:T(8,128)(2,1)S(1)} %all_to_all.45.points_ref, bf16[256,256]{1,0:T(8,128)(2,1)S(1)} %get-tuple-element.30.wa_ref, bf16[256,256]{1,0:T(8,128)(2,1)S(1)} %get-tuple-element.31.wb_ref), custom_call_target="tpu_custom_call" | custom-call | tf_op jit(solution)/shard_map/pallas_call | solution.py:172
  58.1 0.0 collective-permute-done.points_ref
  58.1 9.7 %shard_map.43.other_ref.refs_4_.refs_5_.refs_6_.refs_7_.refs_8_.refs_9_.refs_10_ = bf16[8,2048,256]{2,1,0:T(8,128)(2,1)S(1)} custom-call(bf16[64,144,128]{2,1,0:T(8,128)(2,1)S(1)} %collective-permute-done.points_ref, bf16[256,256]{1,0:T(8,128)(2,1)S(1)} %get-tuple-element.30.wa_ref, bf16[256,256]{1,0:T(8,128)(2,1)S(1)} %get-tuple-element.31.wb_ref), custom_call_target="tpu_custom_call" | custom-call | tf_op jit(solution)/shard_map/pallas_call | solution.py:172
  67.8 2.6 %shard_map.44 = (f32[256,128]{1,0:T(8,128)S(1)}, f32[2,128]{1,0:T(2,128)S(1)}, f32[128,2,128]{2,1,0:T(2,128)S(1)}) custom-call(bf16[64,16,128]{2,1,0:T(8,128)(2,1)S(1)} %slice.8.mine_vec_ref, bf16[64,16,128]{2,1,0:T(8,128)(2,1)S(1)} %slice.9.other_vec_ref, ...), custom_call_target="tpu_custom_call" | custom-call | tf_op jit(solution)/shard_map/pallas_call | solution.py:172
  70.4 14.0 %all_to_all.46 = f32[128,2,128]{2,1,0:T(2,128)S(1)} all-to-all(f32[128,2,128]{2,1,0:T(2,128)S(1)} %get-tuple-element.32), channel_id=1, replica_groups=mesh['z'=4,'core'=2,'x'=4,'y'=4] {'z','core','x','y'}, dimensions={0} | all-to-all | bytes 262144 | tf_op jit(solution)/shard_map/all_to_all | solution.py:160
  84.4 2.8 %shard_map.45 = (f32[256,128]{1,0:T(8,128)S(1)}, f32[2,128]{1,0:T(2,128)S(1)}, f32[128,2,128]{2,1,0:T(2,128)S(1)}) custom-call(f32[256,128]{1,0:T(8,128)S(1)} %bitcast.10, f32[2,128]{1,0:T(2,128)S(1)} %get-tuple-element.33.refs_1_, f32[256,128]{1,0:T(8,128)S(1)} %get-tuple-element.34.refs_2_, ...), custom_call_target="tpu_custom_call" | custom-call | tf_op jit(solution)/shard_map/pallas_call | solution.py:172
  87.2 14.2 %all_to_all.47 = f32[128,2,128]{2,1,0:T(2,128)S(1)} all-to-all(f32[128,2,128]{2,1,0:T(2,128)S(1)} %get-tuple-element.35), channel_id=1, replica_groups=mesh['z'=4,'core'=2,'x'=4,'y'=4] {'z','core','x','y'}, dimensions={0} | all-to-all | bytes 262144 | tf_op jit(solution)/shard_map/all_to_all | solution.py:160
  101.4 2.8 %shard_map.46 = (f32[256,128]{1,0:T(8,128)S(1)}, f32[2,128]{1,0:T(2,128)S(1)}, f32[128,2,128]{2,1,0:T(2,128)S(1)}) custom-call(f32[256,128]{1,0:T(8,128)S(1)} %bitcast.11, f32[2,128]{1,0:T(2,128)S(1)} %get-tuple-element.36.refs_1_, f32[256,128]{1,0:T(8,128)S(1)} %get-tuple-element.34.refs_2_, f32[256,128]{1,0:T(8,128)S(1)} %get-tuple-element.37.refs_3_, ...), custom_call_target="tpu_custom_call" | custom-call | tf_op jit(solution)/shard_map/pallas_call | solution.py:172
  104.2 14.2 %all_to_all.48 = f32[128,2,128]{2,1,0:T(2,128)S(1)} all-to-all(f32[128,2,128]{2,1,0:T(2,128)S(1)} %get-tuple-element.38), channel_id=1, replica_groups=mesh['z'=4,'core'=2,'x'=4,'y'=4] {'z','core','x','y'}, dimensions={0} | all-to-all | bytes 262144 | tf_op jit(solution)/shard_map/all_to_all | solution.py:160
  118.4 2.8 %shard_map.47 = (f32[256,128]{1,0:T(8,128)S(1)}, f32[2,128]{1,0:T(2,128)S(1)}, f32[128,2,128]{2,1,0:T(2,128)S(1)}) custom-call(f32[256,128]{1,0:T(8,128)S(1)} %bitcast.12, f32[2,128]{1,0:T(2,128)S(1)} %get-tuple-element.39.refs_1_, f32[256,128]{1,0:T(8,128)S(1)} %get-tuple-element.34.refs_2_, f32[256,128]{1,0:T(8,128)S(1)} %get-tuple-element.37.refs_3_, ...), custom_call_target="tpu_custom_call" | custom-call | tf_op jit(solution)/shard_map/pallas_call | solution.py:172
  121.2 14.2 %all_to_all.49 = f32[128,2,128]{2,1,0:T(2,128)S(1)} all-to-all(f32[128,2,128]{2,1,0:T(2,128)S(1)} %get-tuple-element.41), channel_id=1, replica_groups=mesh['z'=4,'core'=2,'x'=4,'y'=4] {'z','core','x','y'}, dimensions={0} | all-to-all | bytes 262144 | tf_op jit(solution)/shard_map/all_to_all | solution.py:160
  135.4 2.9 %shard_map.48 = (f32[256,128]{1,0:T(8,128)S(1)}, f32[2,128]{1,0:T(2,128)S(1)}, f32[128,2,128]{2,1,0:T(2,128)S(1)}) custom-call(f32[256,128]{1,0:T(8,128)S(1)} %bitcast.13, f32[2,128]{1,0:T(2,128)S(1)} %get-tuple-element.42.refs_1_, f32[256,128]{1,0:T(8,128)S(1)} %get-tuple-element.34.refs_2_, f32[256,128]{1,0:T(8,128)S(1)} %get-tuple-element.37.refs_3_, ...), custom_call_target="tpu_custom_call" | custom-call | tf_op jit(solution)/shard_map/pallas_call | solution.py:172
  138.3 14.2 %all_to_all.50 = f32[128,2,128]{2,1,0:T(2,128)S(1)} all-to-all(f32[128,2,128]{2,1,0:T(2,128)S(1)} %get-tuple-element.44), channel_id=1, replica_groups=mesh['z'=4,'core'=2,'x'=4,'y'=4] {'z','core','x','y'}, dimensions={0} | all-to-all | bytes 262144 | tf_op jit(solution)/shard_map/all_to_all | solution.py:160
  152.5 2.9 %shard_map.49 = (f32[256,128]{1,0:T(8,128)S(1)}, f32[2,128]{1,0:T(2,128)S(1)}, f32[128,2,128]{2,1,0:T(2,128)S(1)}) custom-call(f32[256,128]{1,0:T(8,128)S(1)} %bitcast.14, f32[2,128]{1,0:T(2,128)S(1)} %get-tuple-element.45.refs_1_, f32[256,128]{1,0:T(8,128)S(1)} %get-tuple-element.34.refs_2_, f32[256,128]{1,0:T(8,128)S(1)} %get-tuple-element.37.refs_3_, ...), custom_call_target="tpu_custom_call" | custom-call | tf_op jit(solution)/shard_map/pallas_call | solution.py:172
  155.3 14.2 %all_to_all.51 = f32[128,2,128]{2,1,0:T(2,128)S(1)} all-to-all(f32[128,2,128]{2,1,0:T(2,128)S(1)} %get-tuple-element.47), channel_id=1, replica_groups=mesh['z'=4,'core'=2,'x'=4,'y'=4] {'z','core','x','y'}, dimensions={0} | all-to-all | bytes 262144 | tf_op jit(solution)/shard_map/all_to_all | solution.py:160
  169.5 2.9 %shard_map.50 = (f32[256,128]{1,0:T(8,128)S(1)}, f32[2,128]{1,0:T(2,128)S(1)}, f32[128,2,128]{2,1,0:T(2,128)S(1)}) custom-call(f32[256,128]{1,0:T(8,128)S(1)} %bitcast.15, f32[2,128]{1,0:T(2,128)S(1)} %get-tuple-element.48.refs_1_, f32[256,128]{1,0:T(8,128)S(1)} %get-tuple-element.34.refs_2_, f32[256,128]{1,0:T(8,128)S(1)} %get-tuple-element.37.refs_3_, ...), custom_call_target="tpu_custom_call" | custom-call | tf_op jit(solution)/shard_map/pallas_call | solution.py:172
  172.5 14.2 %all_to_all.52 = f32[128,2,128]{2,1,0:T(2,128)S(1)} all-to-all(f32[128,2,128]{2,1,0:T(2,128)S(1)} %get-tuple-element.50), channel_id=1, replica_groups=mesh['z'=4,'core'=2,'x'=4,'y'=4] {'z','core','x','y'}, dimensions={0} | all-to-all | bytes 262144 | tf_op jit(solution)/shard_map/all_to_all | solution.py:160
  186.7 3.0 %shard_map.51 = (f32[256,128]{1,0:T(8,128)S(1)}, f32[2,128]{1,0:T(2,128)S(1)}, f32[128,2,128]{2,1,0:T(2,128)S(1)}) custom-call(f32[256,128]{1,0:T(8,128)S(1)} %bitcast.9, f32[2,128]{1,0:T(2,128)S(1)} %get-tuple-element.51.refs_1_, f32[256,128]{1,0:T(8,128)S(1)} %get-tuple-element.34.refs_2_, f32[256,128]{1,0:T(8,128)S(1)} %get-tuple-element.37.refs_3_, ...), custom_call_target="tpu_custom_call" | custom-call | tf_op jit(solution)/shard_map/pallas_call | solution.py:172
  189.6 14.2 %all_to_all.53 = f32[128,2,128]{2,1,0:T(2,128)S(1)} all-to-all(f32[128,2,128]{2,1,0:T(2,128)S(1)} %get-tuple-element.53), channel_id=1, replica_groups=mesh['z'=4,'core'=2,'x'=4,'y'=4] {'z','core','x','y'}, dimensions={0} | all-to-all | bytes 262144 | tf_op jit(solution)/shard_map/all_to_all | solution.py:160
  203.8 1.4 shard_map.52
  (2 shorter events, 0.0 us)
Async XLA Ops:
  0.6 0.8 copy-start
  1.5 0.7 copy-start.1
  46.2 11.9 %collective-permute-start = (bf16[64,144,128]{2,1,0:T(8,128)(2,1)S(1)}, bf16[64,144,128]{2,1,0:T(8,128)(2,1)S(1)}, u32[]{:S(2)}, u32[]{:S(2)}) collective-permute-start(bf16[64,144,128]{2,1,0:T(8,128)(2,1)S(1)} %all_to_all.45.points_ref), channel_id=1, source_target_pairs={{0,16},{16,0},{1,17},{17,1},{2,18},{18,2},{3,19},{19,3},{4,20},{20... | collective-permute-start | bytes 7077896 | tf_op jit(solution)/shard_map/ppermute | solution.py:194
